TPU v7x, 32 devices: a whole 2x2x4 slice. The times are simulated.
32 devices in a mesh: ep: 4 (over y, x), fsdp: 8 (over z, core).
Axes of the slice: x: 2, y: 2, z: 4, core: 2. Of those that a mesh axis runs over, the one named last changes fastest.
Arguments:
- w_gate: float32 [64, 2048, 1024], P('ep', 'fsdp'), may hold values from -0.1875 to 0.1875
- avg_gate: bfloat16 [64, 2048, 1024], P('ep', 'fsdp'), may hold values from -0.0625 to 0.0625
- w_up: float32 [64, 2048, 1024], P('ep', 'fsdp'), may hold values from -0.1875 to 0.1875
- avg_up: bfloat16 [64, 2048, 1024], P('ep', 'fsdp'), may hold values from -0.0625 to 0.0625
- w_down: float32 [64, 1024, 2048], P('ep', None, 'fsdp'), may hold values from -0.25 to 0.25
- avg_down: bfloat16 [64, 1024, 2048], P('ep', None, 'fsdp'), may hold values from -0.09375 to 0.09375
- router_weight: float32 [2048, 64], P('fsdp', 'ep'), may hold values from -0.125 to 0.125
- router_gain: float32 [2048], P('fsdp'), may hold values from 0.25 to 1.75
Outputs:
- serve_gate: bfloat16 [64, 2048, 1024], P('ep', None, 'fsdp')
- serve_up: bfloat16 [64, 2048, 1024], P('ep', None, 'fsdp')
- serve_down: bfloat16 [64, 1024, 2048], P('ep', 'fsdp')
- scale_gate: float32 [64, 1024], P('ep', 'fsdp')
- scale_up: float32 [64, 1024], P('ep', 'fsdp')
- scale_down: float32 [64, 1024], P('ep', 'fsdp')
- serve_router: bfloat16 [2048, 64], replicated
All inputs are finite; a program needn't handle non-finite values.
Results may differ from a plain program's by a relative error of at most 0.001.
Values may be sent and summed in bfloat16 or wider, within the bound.
A program may use at most 192 MiB of HBM per device.

v0:
```python
import jax
import jax.numpy as jnp
from jax import lax
from jax.experimental import pallas as pl
from jax.sharding import PartitionSpec as P


def fresh_of(w, avg):
    return w + avg.astype(jnp.float32)


def narrow_of(w, avg, total, axis):
    return (fresh_of(w, avg) / jnp.expand_dims(jnp.sqrt(total), axis)).astype(jnp.bfloat16)


def squares(w, avg, axis):
    fresh = fresh_of(w, avg)
    return jnp.sum(fresh * fresh, axis=axis)


def exchange(x):
    return lax.all_to_all(x, "fsdp", split_axis=0, concat_axis=0, tiled=True)


def sum_kernel(w_ref, avg_ref, total_ref):
    fresh = w_ref[0] + avg_ref[0].astype(jnp.float32)
    total_ref[0] = jnp.sum(fresh * fresh, axis=0, keepdims=True)


def piece_kernel(n, w_ref, avg_ref, total_ref, out_ref):
    width = w_ref.shape[2] // n
    for k in range(n):
        at = slice(k * width, (k + 1) * width)
        fresh = w_ref[0, :, at] + avg_ref[0, :, at].astype(jnp.float32)
        out_ref[k, 0] = (fresh / jnp.sqrt(total_ref[0, :, at])).astype(jnp.bfloat16)


def column_squares(w, avg):
    experts, depth, width = w.shape
    block = pl.BlockSpec((1, depth, width), lambda e: (e, 0, 0))
    total = pl.pallas_call(
        sum_kernel,
        grid=(experts,),
        in_specs=[block, block],
        out_specs=pl.BlockSpec((1, 1, width), lambda e: (e, 0, 0)),
        out_shape=jax.ShapeDtypeStruct((experts, 1, width), jnp.float32),
        cost_estimate=pl.CostEstimate(flops=3 * w.size, bytes_accessed=6 * w.size, transcendentals=0),
    )(w, avg)
    return total.reshape(experts, width)


def column_pieces(w, avg, total):
    n = lax.axis_size("fsdp")
    experts, depth, width = w.shape
    block = pl.BlockSpec((1, depth, width), lambda e: (e, 0, 0))
    return pl.pallas_call(
        lambda *refs: piece_kernel(n, *refs),
        grid=(experts,),
        in_specs=[block, block, pl.BlockSpec((1, 1, width), lambda e: (e, 0, 0))],
        out_specs=pl.BlockSpec((n, 1, depth, width // n), lambda e: (0, e, 0, 0)),
        out_shape=jax.ShapeDtypeStruct((n, experts, depth, width // n), jnp.bfloat16),
        cost_estimate=pl.CostEstimate(flops=3 * w.size, bytes_accessed=8 * w.size, transcendentals=0),
    )(w, avg, total.reshape(experts, 1, width))


def columns(pieces):
    n, experts, depth, width = pieces.shape
    return exchange(pieces).transpose(1, 0, 2, 3).reshape(experts, n * depth, width)


def join_kernel(in_ref, out_ref):
    n, _, _, depth = in_ref.shape
    for k in range(n):
        out_ref[0, :, k * depth : (k + 1) * depth] = in_ref[k, 0]


def rows(x):
    n = lax.axis_size("fsdp")
    experts, height, depth = x.shape
    part = height // n
    pieces = exchange(x.reshape(experts, n, part, depth).transpose(1, 0, 2, 3))
    return pl.pallas_call(
        join_kernel,
        grid=(experts,),
        in_specs=[pl.BlockSpec((n, 1, part, depth), lambda e: (0, e, 0, 0))],
        out_specs=pl.BlockSpec((1, part, n * depth), lambda e: (e, 0, 0)),
        out_shape=jax.ShapeDtypeStruct((experts, part, n * depth), x.dtype),
        cost_estimate=pl.CostEstimate(flops=0, bytes_accessed=4 * x.size, transcendentals=0),
    )(pieces)


def on_device(w_gate, avg_gate, w_up, avg_up, w_down, avg_down, router_weight, router_gain):
    part_router = (router_weight * router_gain[:, None]).astype(jnp.bfloat16)
    row_router = lax.all_gather(part_router, "fsdp", axis=0, tiled=True)
    serve_router = lax.all_gather(row_router, "ep", axis=1, tiled=True)
    total_gate = lax.psum(column_squares(w_gate, avg_gate), "fsdp")
    total_gate, serve_router = lax.optimization_barrier((total_gate, serve_router))
    gate = column_pieces(w_gate, avg_gate, total_gate)
    gate, late_up, late_down = lax.optimization_barrier((gate, avg_up, avg_down))
    serve_gate = columns(gate)
    square_up, square_down = column_squares(w_up, late_up), squares(w_down, late_down, 2)
    total_up, total_down = lax.psum((square_up, square_down), "fsdp")
    up = column_pieces(w_up, avg_up, total_up)
    up, total_down = lax.optimization_barrier((up, total_down))
    serve_up = columns(up)
    serve_down = rows(narrow_of(w_down, avg_down, total_down, 2))

    def own(total, width):
        return jnp.sqrt(
            lax.dynamic_slice_in_dim(total, lax.axis_index("fsdp") * width, width, axis=1)
        )

    scale_gate = own(total_gate, serve_gate.shape[2])
    scale_up = own(total_up, serve_up.shape[2])
    scale_down = own(total_down, serve_down.shape[1])
    return (serve_gate, serve_up, serve_down, scale_gate, scale_up, scale_down, serve_router)


def solution(mesh):
    placed = (
        P("ep", "fsdp", None),
        P("ep", "fsdp", None),
        P("ep", "fsdp", None),
        P("ep", "fsdp", None),
        P("ep", None, "fsdp"),
        P("ep", None, "fsdp"),
        P("fsdp", "ep"),
        P("fsdp"),
    )
    return jax.shard_map(
        on_device,
        mesh=mesh,
        in_specs=placed,
        out_specs=(
            P("ep", None, "fsdp"),
            P("ep", None, "fsdp"),
            P("ep", "fsdp", None),
            P("ep", "fsdp"),
            P("ep", "fsdp"),
            P("ep", "fsdp"),
            P(),
        ),
        check_vma=False,
    )
```

profile of v0, /device:TPU:9, one launch (start us, length us, event | category | flops | bytes accessed | tf_op | source)
XLA Modules:
  0.0 683.9 jit_solution(17806020933095240582)
XLA Ops:
  7.2 0.0 copy-start.2
  7.2 0.0 copy-start.1
  7.2 0.0 all-reduce.4.cloned.1.call-start
  7.2 14.9 %shard_map.135 = f32[16,1,1024]{2,1,0:T(1,128)} custom-call(f32[16,256,1024]{2,1,0:T(8,128)} %refs_0_.2, bf16[16,256,1024]{2,1,0:T(8,128)(2,1)} %refs_1_.2), custom_call_target="tpu_custom_call" | custom-call | flops 12582912 | bytes 25165824 | tf_op jit(solution)/shard_map/pallas_call | solution.py:41
  22.2 1.5 copy.25
  23.7 0.0 all-reduce.4.cloned.1.call-update
  23.7 0.0 copy-done.2
  23.7 0.0 copy-done.1
  23.7 14.7 %all_gather.6 = bf16[2048,16]{0,1:T(8,128)(2,1)S(1)} all-gather(bf16[256,16]{0,1:T(8,128)(2,1)S(1)} %multiply_convert_fusion), channel_id=1, replica_groups=mesh['ep'=4,'fsdp'=8] {'fsdp'}, dimensions={0}, use_global_device_ids=true | all-gather | bytes 73728 | tf_op jit(solution)/shard_map/all_gather | solution.py:94
  38.4 7.0 %all_gather.7 = bf16[2048,64]{0,1:T(8,128)(2,1)S(1)} all-gather(bf16[2048,16]{0,1:T(8,128)(2,1)S(1)} %all_gather.6), channel_id=1, replica_groups=mesh['ep'=4,'fsdp'=8] {'ep'}, dimensions={1}, use_global_device_ids=true | all-gather | bytes 327680 | tf_op jit(solution)/shard_map/all_gather | solution.py:95
  45.5 31.9 %all-reduce.4.cloned.1.call-done = f32[16,1024]{1,0:T(8,128)} async-done(((f32[16,1024]{1,0:T(8,128)}), f32[16,1024]{1,0:T(8,128)}) %all-reduce.4.cloned.1.call-update) | async-done | bytes 65552 | tf_op jit(solution)/shard_map/psum | solution.py:96
  77.4 1.5 reshape.38.refs_2_
  78.9 17.0 %shard_map.136 = bf16[8,16,256,128]{3,2,1,0:T(8,128)(2,1)} custom-call(f32[16,256,1024]{2,1,0:T(8,128)} %refs_0_.2, bf16[16,256,1024]{2,1,0:T(8,128)(2,1)} %refs_1_.2, f32[16,1,1024]{2,1,0:T(1,128)} %reshape.38.refs_2_), custom_call_target="tpu_custom_call" | custom-call | flops 12582912 | bytes 33554432 | tf_op jit(solution)/shard_map/pallas_call | solution.py:56
  95.9 8.0 %all-to-all-start = ((bf16[8,16,256,128]{3,2,1,0:T(8,128)(2,1)}), bf16[8,16,256,128]{3,2,1,0:T(8,128)(2,1)}, u32[]{:S(2)}, u32[]{:S(2)}) async-start(bf16[8,16,256,128]{3,2,1,0:T(8,128)(2,1)} %shard_map.136), calls=%async_computation | async-start | bytes 16777216 | tf_op jit(solution)/shard_map/all_to_all | solution.py:22
  103.9 0.0 all-reduce.6.cloned.1.call-start
  103.9 14.9 %shard_map.137 = f32[16,1,1024]{2,1,0:T(1,128)} custom-call(f32[16,256,1024]{2,1,0:T(8,128)} %refs_0_.3, bf16[16,256,1024]{2,1,0:T(8,128)(2,1)} %refs_1_.3), custom_call_target="tpu_custom_call" | custom-call | flops 12582912 | bytes 25165824 | tf_op jit(solution)/shard_map/pallas_call | solution.py:41
  118.8 1.5 copy.24
  120.3 9.7 %multiply_reduce_fusion = f32[16,1024]{1,0:T(8,128)} fusion(f32[16,1024,256]{2,1,0:T(8,128)} %param.12, bf16[16,1024,256]{2,1,0:T(8,128)(2,1)} %param.13), kind=kLoop, calls=%fused_computation.1 | loop fusion | flops 16760832 | bytes 25231360 | tf_op jit(solution)/shard_map/reduce_sum | solution.py:18
  130.0 0.0 all-reduce.6.cloned.1.call-update
  130.0 55.0 %all-reduce.6.cloned.1.call-done = (f32[16,1024]{1,0:T(8,128)}, f32[16,1024]{1,0:T(8,128)}) async-done(((f32[16,1024]{1,0:T(8,128)}, f32[16,1024]{1,0:T(8,128)}), (f32[16,1024]{1,0:T(8,128)}, f32[16,1024]{1,0:T(8,128)})) %all-reduce.6.cloned.1.call-update) | async-done | bytes 131088 | tf_op jit(solution)/shard_map/psum | solution.py:102
  185.0 1.5 reshape.41.refs_2_
  186.5 17.0 %shard_map.138 = bf16[8,16,256,128]{3,2,1,0:T(8,128)(2,1)} custom-call(f32[16,256,1024]{2,1,0:T(8,128)} %refs_0_.3, bf16[16,256,1024]{2,1,0:T(8,128)(2,1)} %refs_1_.3, f32[16,1,1024]{2,1,0:T(1,128)} %reshape.41.refs_2_), custom_call_target="tpu_custom_call" | custom-call | flops 12582912 | bytes 33554432 | tf_op jit(solution)/shard_map/pallas_call | solution.py:56
  203.6 0.0 copy-start
  203.6 83.1 %all-to-all-done = bf16[8,16,256,128]{3,2,1,0:T(8,128)(2,1)} async-done(((bf16[8,16,256,128]{3,2,1,0:T(8,128)(2,1)}), bf16[8,16,256,128]{3,2,1,0:T(8,128)(2,1)}, u32[]{:S(2)}, u32[]{:S(2)}) %all-to-all-start) | async-done | bytes 8388640 | tf_op jit(solution)/shard_map/all_to_all | solution.py:22
  286.7 8.5 %all-to-all-start.1 = ((bf16[8,16,256,128]{3,2,1,0:T(8,128)(2,1)}), bf16[8,16,256,128]{3,2,1,0:T(8,128)(2,1)}, u32[]{:S(2)}, u32[]{:S(2)}) async-start(bf16[8,16,256,128]{3,2,1,0:T(8,128)(2,1)} %shard_map.138), calls=%async_computation.1 | async-start | bytes 16777216 | tf_op jit(solution)/shard_map/all_to_all | solution.py:22
  295.2 0.0 copy-done
  295.2 12.0 %divide_convert_fusion = bf16[16,1024,256]{2,1,0:T(8,128)(2,1)} fusion(f32[16,1024,256]{2,1,0:T(8,128)} %param.12, bf16[16,1024,256]{2,1,0:T(8,128)(2,1)} %param.13, f32[16,1024]{1,0:T(8,128)S(1)} %sqrt.12), kind=kLoop, calls=%fused_computation | loop fusion | flops 16777216 | bytes 33619968 | tf_op jit(solution)/shard_map/convert_element_type | solution.py:13
  307.2 7.7 %copy.23 = bf16[16,8,128,256]{3,2,0,1:T(8,128)(2,1)} copy(bf16[16,8,128,256]{3,2,1,0:T(8,128)(2,1)} %bitcast.15) | data formatting | bytes 16777216 | tf_op jit(solution)/shard_map/reshape | solution.py:81
  314.9 160.6 %all-to-all-done.1 = bf16[8,16,256,128]{3,2,1,0:T(8,128)(2,1)} async-done(((bf16[8,16,256,128]{3,2,1,0:T(8,128)(2,1)}), bf16[8,16,256,128]{3,2,1,0:T(8,128)(2,1)}, u32[]{:S(2)}, u32[]{:S(2)}) %all-to-all-start.1) | async-done | bytes 8388640 | tf_op jit(solution)/shard_map/all_to_all | solution.py:22
  475.6 8.5 %all-to-all-start.2 = ((bf16[8,16,128,256]{3,2,1,0:T(8,128)(2,1)}), bf16[8,16,128,256]{3,2,1,0:T(8,128)(2,1)}, u32[]{:S(2)}, u32[]{:S(2)}) async-start(bf16[8,16,128,256]{3,2,1,0:T(8,128)(2,1)} %bitcast.14), calls=%async_computation.2 | async-start | bytes 16777216 | tf_op jit(solution)/shard_map/all_to_all | solution.py:22
  484.0 1.3 dynamic-slice_sqrt_fusion.2
  485.3 1.3 dynamic-slice_sqrt_fusion
  486.6 7.9 %copy.15 = bf16[16,8,256,128]{3,2,1,0:T(8,128)(2,1)} copy(bf16[16,8,256,128]{3,2,0,1:T(8,128)(2,1)} %bitcast) | data formatting | bytes 16777216 | tf_op jit(solution)/shard_map/transpose | solution.py:68
  494.5 7.9 %copy.16 = bf16[16,8,256,128]{3,2,1,0:T(8,128)(2,1)} copy(bf16[16,8,256,128]{3,2,0,1:T(8,128)(2,1)} %bitcast.2) | data formatting | bytes 16777216 | tf_op jit(solution)/shard_map/transpose | solution.py:68
  502.4 162.0 %all-to-all-done.2.in_ref = bf16[8,16,128,256]{3,2,1,0:T(8,128)(2,1)} async-done(((bf16[8,16,128,256]{3,2,1,0:T(8,128)(2,1)}), bf16[8,16,128,256]{3,2,1,0:T(8,128)(2,1)}, u32[]{:S(2)}, u32[]{:S(2)}) %all-to-all-start.2) | async-done | bytes 8388640 | tf_op jit(solution)/shard_map/all_to_all | solution.py:22
  664.4 12.0 %shard_map.139 = bf16[16,128,2048]{2,1,0:T(8,128)(2,1)} custom-call(bf16[8,16,128,256]{3,2,1,0:T(8,128)(2,1)} %all-to-all-done.2.in_ref), custom_call_target="tpu_custom_call" | custom-call | bytes 16777216 | tf_op jit(solution)/shard_map/pallas_call | solution.py:82
  676.4 0.7 copy.30
  (2 shorter events, 0.0 us)
Async XLA Ops:
  7.2 16.5 %copy-start.2 = (f32[256]{0:T(256)S(1)}, f32[256]{0:T(256)}, u32[]{:S(2)}) copy-start(f32[256]{0:T(256)} %param.15) | copy-start | bytes 3076
  7.2 16.5 %copy-start.1 = (f32[256,16]{0,1:T(8,128)S(1)}, f32[256,16]{0,1:T(8,128)}, u32[]{:S(2)}) copy-start(f32[256,16]{0,1:T(8,128)} %param.14) | copy-start | bytes 49156
  7.2 70.2 %all-reduce.4.cloned.1.call-start = ((), (), s32[]{:S(2)}) async-start(), calls=%async_computation.3 | async-start | bytes 131072 | tf_op jit(solution)/shard_map/psum | solution.py:96
  95.9 190.8 %all-to-all-start = ((bf16[8,16,256,128]{3,2,1,0:T(8,128)(2,1)}), bf16[8,16,256,128]{3,2,1,0:T(8,128)(2,1)}, u32[]{:S(2)}, u32[]{:S(2)}) async-start(bf16[8,16,256,128]{3,2,1,0:T(8,128)(2,1)} %shard_map.136), calls=%async_computation | async-start | bytes 16777216 | tf_op jit(solution)/shard_map/all_to_all | solution.py:22
  103.9 81.2 %all-reduce.6.cloned.1.call-start = ((), (), s32[]{:S(2)}) async-start(), calls=%async_computation.4 | async-start | bytes 262144 | tf_op jit(solution)/shard_map/psum | solution.py:102
  203.6 91.7 %copy-start = (f32[16,1024]{1,0:T(8,128)S(1)}, f32[16,1024]{1,0:T(8,128)}, u32[]{:S(2)}) copy-start(f32[16,1024]{1,0:T(8,128)} %get-tuple-element.19) | copy-start | bytes 196612
  286.7 188.9 %all-to-all-start.1 = ((bf16[8,16,256,128]{3,2,1,0:T(8,128)(2,1)}), bf16[8,16,256,128]{3,2,1,0:T(8,128)(2,1)}, u32[]{:S(2)}, u32[]{:S(2)}) async-start(bf16[8,16,256,128]{3,2,1,0:T(8,128)(2,1)} %shard_map.138), calls=%async_computation.1 | async-start | bytes 16777216 | tf_op jit(solution)/shard_map/all_to_all | solution.py:22
  475.6 188.8 %all-to-all-start.2 = ((bf16[8,16,128,256]{3,2,1,0:T(8,128)(2,1)}), bf16[8,16,128,256]{3,2,1,0:T(8,128)(2,1)}, u32[]{:S(2)}, u32[]{:S(2)}) async-start(bf16[8,16,128,256]{3,2,1,0:T(8,128)(2,1)} %bitcast.14), calls=%async_computation.2 | async-start | bytes 16777216 | tf_op jit(solution)/shard_map/all_to_all | solution.py:22
Sparse Core Ops, SparseCore 0:
  23.8 53.5 all-reduce.3
  130.2 54.8 all-reduce.5
where the time goes:
time: 690 us; the launch traced here: 684 us
  waiting for transfers between devices  493 us (71%)
  Pallas kernels  75.9 us (11%)
  local copies, waits for them, and re-layouts  32.8 us (5%)
  starting transfers between devices  25 us (4%)
  blocking collectives  21.8 us (3%)
  other arithmetic  21.7 us (3%)
  between operations  14.1 us (2%)
    all_to_all x3, waiting for transfers between devices, exchange(): return lax.all_to_all(x, 'fsdp', split_axis=0, concat_axis=0, tiled=True)  406 us
    psum x1, waiting for transfers between devices, on_device(): total_up, total_down = lax.psum((square_up, square_down), 'fsdp')  55 us
    pallas_call x2, Pallas kernels, column_pieces(): pl.pallas_call(lambda *refs: piece_kernel(n, *refs), grid=(experts,), in_...  34 us
    psum x1, waiting for transfers between devices, on_device(): total_gate = lax.psum(column_squares(w_gate, avg_gate), 'fsdp')  31.9 us
    pallas_call x2, Pallas kernels, column_squares(): pl.pallas_call(sum_kernel, grid=(experts,), in_specs=[block, block], out_...  29.9 us
    all_to_all x3, starting transfers between devices, exchange(): return lax.all_to_all(x, 'fsdp', split_axis=0, concat_axis=0, tiled=True)  25 us
    transpose x2, local copies, waits for them, and re-layouts, columns(): exchange(pieces).transpose(1, 0, 2, 3).reshape(experts, n * depth, width)  15.8 us
    all_gather x1, blocking collectives, on_device(): row_router = lax.all_gather(part_router, 'fsdp', axis=0, tiled=True)  14.7 us
  transfers between devices with their start and end apart: 5, of which 5 were waited for; matrix products, arithmetic and copies ran while one was open for 7% of the time, Pallas kernels for 5%

commit v1 on v0

v1 whole, which is shorter than its diff:
```python
import functools

import jax
import jax.numpy as jnp
from jax import lax
from jax.experimental import pallas as pl
from jax.experimental.pallas import tpu as pltpu
from jax.sharding import PartitionSpec as P

MESH = pl.DeviceIdType.MESH
MIB = 1 << 20
SLOTS = 4
RING = 8
LANES = 128


def chunks_of(experts):
    first = max(1, experts // 8)
    early = max(first, experts // 2)
    return first, early


def fresh_of(w, avg):
    return w + avg.astype(jnp.float32)


def work_kernel(
    wg_ref, ag_ref, wu_ref, au_ref, wd_ref, ad_ref, rw_ref, gain_ref,
    og_ref, ou_ref, od_ref, scale_ref, router_ref,
    wide_w, wide_avg, tall_w, tall_avg, wide_stage, tall_stage,
    part_a, part_b, part_c, sums_a, sums_b, sums_c, inv_a, inv_b, inv_c, own_router,
    wide_sem, tall_sem, wide_sent, tall_sent, landed,
    sums_sent, sums_landed, inv_sent, inv_landed, router_sent, router_landed,
):
    n, ep = lax.axis_size("fsdp"), lax.axis_size("ep")
    me, group = lax.axis_index("fsdp"), lax.axis_index("ep")
    experts, depth, d_expert = wg_ref.shape
    width = d_expert // n
    first, early = chunks_of(experts)

    barrier = pltpu.get_barrier_semaphore()
    for d in range(1, n):
        pl.semaphore_signal(
            barrier, inc=1, device_id={"fsdp": lax.rem(me + d, n)}, device_id_type=MESH
        )
    for d in range(1, ep):
        pl.semaphore_signal(
            barrier, inc=1, device_id={"ep": lax.rem(group + d, ep)}, device_id_type=MESH
        )

    gate = (wg_ref, ag_ref, wide_w, wide_avg, wide_sem)
    up = (wu_ref, au_ref, wide_w, wide_avg, wide_sem)
    down = (wd_ref, ad_ref, tall_w, tall_avg, tall_sem)

    def loads(m, e, slot):
        w, avg, w_buf, avg_buf, sem = m
        return (
            pltpu.make_async_copy(w.at[e], w_buf.at[slot], sem.at[slot, 0]),
            pltpu.make_async_copy(avg.at[e], avg_buf.at[slot], sem.at[slot, 1]),
        )

    def prime(m, start, stop):
        for i in range(min(SLOTS, stop - start)):
            for copy in loads(m, start + i, i):
                copy.start()

    def stream(m, start, stop, body):
        count = stop - start

        def step(i, carry):
            slot = lax.rem(i, SLOTS)
            for copy in loads(m, start + i, slot):
                copy.wait()
            body(start + i, slot)

            @pl.when(i + SLOTS < count)
            def _():
                for copy in loads(m, start + i + SLOTS, slot):
                    copy.start()

            return carry

        lax.fori_loop(0, count, step, 0)

    def column_sums(part, shift, e, slot):
        for k in range(n):
            at = slice(k * width, (k + 1) * width)
            fresh = fresh_of(wide_w[slot, :, at], wide_avg[slot, :, at])
            part[k, pl.ds(e + shift, 1), :] = jnp.sum(fresh * fresh, axis=0, keepdims=True)

    def row_sums(part, shift, e, slot):
        span = tall_w.shape[2]
        for k in range(n):
            at = slice(k * width, (k + 1) * width)
            total = None
            for c in range(span // LANES):
                lanes = slice(c * LANES, (c + 1) * LANES)
                fresh = fresh_of(tall_w[slot, at, lanes], tall_avg[slot, at, lanes])
                total = fresh * fresh if total is None else total + fresh * fresh
            part[k, pl.ds(e + shift, 1), :] = jnp.sum(total.T, axis=0, keepdims=True)

    def to_all(send):
        for d in range(1, n):
            send(lax.rem(me + d, n))

    def send_sums(chunk, part, sums):
        sums[me] = part[me]

        def send(k):
            pltpu.make_async_remote_copy(
                src_ref=part.at[k], dst_ref=sums.at[me],
                send_sem=sums_sent.at[chunk], recv_sem=sums_landed.at[chunk],
                device_id={"fsdp": k}, device_id_type=MESH,
            ).start()

        to_all(send)

    def others(ref, sem):
        some = ref.at[pl.ds(0, n - 1)]
        return pltpu.make_async_copy(some, some, sem)

    def send_inverse(chunk, sums, inv, places):
        others(sums, sums_landed.at[chunk]).wait()
        total = sums[0]
        for k in range(1, n):
            total = total + sums[k]
        scale = jnp.sqrt(total)
        at = 0
        for m, start, stop in places:
            scale_ref[m, start:stop] = scale[at : at + stop - start]
            at += stop - start
        inv[me] = 1.0 / scale

        def send(k):
            pltpu.make_async_remote_copy(
                src_ref=inv.at[me], dst_ref=inv.at[me],
                send_sem=inv_sent.at[chunk], recv_sem=inv_landed.at[chunk],
                device_id={"fsdp": k}, device_id_type=MESH,
            ).start()

        to_all(send)

    def ring_slot(stage, sent, count):
        ring = lax.rem(count, RING)

        @pl.when(count >= RING)
        def _():
            others(stage.at[ring], sent.at[ring]).wait()

        return ring

    def wide_pieces(m, out, inv, shift, e, slot):
        ring = ring_slot(wide_stage, wide_sent, m * experts + e)
        for k in range(n):
            at = slice(k * width, (k + 1) * width)
            fresh = fresh_of(wide_w[slot, :, at], wide_avg[slot, :, at])
            wide_stage[ring, k] = (fresh * inv[k, pl.ds(e + shift, 1), :]).astype(jnp.bfloat16)
        rows = pl.ds(pl.multiple_of(me * depth, depth), depth)

        def send(k):
            pltpu.make_async_remote_copy(
                src_ref=wide_stage.at[ring, k], dst_ref=out.at[e, rows],
                send_sem=wide_sent.at[ring], recv_sem=landed.at[m, e],
                device_id={"fsdp": k}, device_id_type=MESH,
            ).start()

        to_all(send)
        out[e, rows] = wide_stage[ring, me]

    def tall_pieces(inv, shift, e, slot):
        ring = ring_slot(tall_stage, tall_sent, e)
        span = tall_w.shape[2]
        for k in range(n):
            at = slice(k * width, (k + 1) * width)
            row = inv[k, pl.ds(e + shift, 1), :]
            factor = jnp.broadcast_to(row, (LANES, width)).T
            for c in range(span // LANES):
                lanes = slice(c * LANES, (c + 1) * LANES)
                fresh = fresh_of(tall_w[slot, at, lanes], tall_avg[slot, at, lanes])
                tall_stage[ring, k, :, lanes] = (fresh * factor).astype(jnp.bfloat16)
        columns = pl.ds(pl.multiple_of(me * span, span), span)

        def send(k):
            pltpu.make_async_remote_copy(
                src_ref=tall_stage.at[ring, k], dst_ref=od_ref.at[e, :, columns],
                send_sem=tall_sent.at[ring], recv_sem=landed.at[2, e],
                device_id={"fsdp": k}, device_id_type=MESH,
            ).start()

        to_all(send)
        od_ref[e, :, columns] = tall_stage[ring, me]

    prime(gate, 0, first)
    own_router[...] = (rw_ref[...] * gain_ref[...]).astype(jnp.bfloat16)
    pl.semaphore_wait(barrier, n - 1 + ep - 1)

    stream(gate, 0, first, functools.partial(column_sums, part_a, 0))
    prime(gate, first, early)
    send_sums(0, part_a, sums_a)
    stream(gate, first, early, functools.partial(column_sums, part_b, -first))
    prime(gate, 0, first)
    send_sums(1, part_b, sums_b)
    send_inverse(0, sums_a, inv_a, ((0, 0, first),))

    my_columns = pl.ds(pl.multiple_of(me * depth, depth), depth)

    def send_router(k):
        pltpu.make_async_remote_copy(
            src_ref=own_router, dst_ref=router_ref.at[group, :, my_columns],
            send_sem=router_sent.at[0], recv_sem=router_landed.at[0],
            device_id={"fsdp": k}, device_id_type=MESH,
        ).start()

    def router_wait(sem):
        some = router_ref.at[group, :, pl.ds(0, (n - 1) * depth)]
        return pltpu.make_async_copy(some, some, sem)

    send_inverse(1, sums_b, inv_b, ((0, first, early),))
    others(inv_a, inv_landed.at[0]).wait()
    stream(gate, 0, first, functools.partial(wide_pieces, 0, og_ref, inv_a, 0))
    pieces_b = functools.partial(wide_pieces, 0, og_ref, inv_b, -first)
    cut_one = first + (early - first + 2) // 3
    cut_two = cut_one + (early - cut_one + 1) // 2
    prime(gate, first, cut_one)
    others(inv_b, inv_landed.at[1]).wait()
    stream(gate, first, cut_one, pieces_b)
    to_all(send_router)
    router_ref[group, :, my_columns] = own_router[...]

    prime(gate, early, experts)
    prime(down, 0, experts)
    stream(gate, early, experts, functools.partial(column_sums, part_c, -early))
    rest = experts - early
    prime(up, 0, experts)
    stream(up, 0, experts, functools.partial(column_sums, part_c, rest))
    stream(down, 0, experts, functools.partial(row_sums, part_c, rest + experts))
    send_sums(2, part_c, sums_c)
    prime(gate, cut_one, cut_two)
    stream(gate, cut_one, cut_two, pieces_b)

    router_wait(router_landed.at[0]).wait()
    for d in range(1, ep):
        pltpu.make_async_remote_copy(
            src_ref=router_ref.at[group], dst_ref=router_ref.at[group],
            send_sem=router_sent.at[1], recv_sem=router_landed.at[1],
            device_id={"ep": lax.rem(group + d, ep)}, device_id_type=MESH,
        ).start()

    send_inverse(
        2, sums_c, inv_c, ((0, early, experts), (1, 0, experts), (2, 0, experts))
    )
    prime(gate, cut_two, early)
    stream(gate, cut_two, early, pieces_b)
    prime(gate, early, experts)
    prime(down, 0, experts)
    others(inv_c, inv_landed.at[2]).wait()
    stream(gate, early, experts, functools.partial(wide_pieces, 0, og_ref, inv_c, -early))
    prime(up, 0, experts)
    stream(up, 0, experts, functools.partial(wide_pieces, 1, ou_ref, inv_c, rest))
    stream(down, 0, experts, functools.partial(tall_pieces, inv_c, rest + experts))

    def finish(e, carry):
        wide = wide_stage.at[0, pl.ds(0, n - 1)]
        tall = tall_stage.at[0, pl.ds(0, n - 1)]
        for m, some in ((0, wide), (1, wide), (2, tall)):
            pltpu.make_async_copy(some, some, landed.at[m, e]).wait()
        return carry

    lax.fori_loop(0, experts, finish, 0)

    def drain(count, stage, sent):
        def step(i, carry):
            others(stage.at[i], sent.at[i]).wait()
            return carry

        lax.fori_loop(0, min(RING, count), step, 0)

    drain(2 * experts, wide_stage, wide_sent)
    drain(experts, tall_stage, tall_sent)
    for chunk, (part, inv) in enumerate(((part_a, inv_a), (part_b, inv_b), (part_c, inv_c))):
        others(part, sums_sent.at[chunk]).wait()
        others(inv, inv_sent.at[chunk]).wait()
    router_wait(router_sent.at[0]).wait()
    if ep > 1:
        some = router_ref.at[pl.ds(0, ep - 1)]
        pltpu.make_async_copy(some, some, router_sent.at[1]).wait()
        pltpu.make_async_copy(some, some, router_landed.at[1]).wait()


def write_kernel(
    g_ref, u_ref, d_ref, scale_ref, router_ref,
    og_ref, ou_ref, od_ref, sg_ref, su_ref, sd_ref, out_router_ref, big, small,
):
    copies = []
    experts = g_ref.shape[0]
    parts = min(4, experts)
    span = experts // parts
    for m, (src, dst) in enumerate(((g_ref, og_ref), (u_ref, ou_ref), (d_ref, od_ref))):
        for i in range(parts):
            at = pl.ds(i * span, span)
            copies.append(pltpu.make_async_copy(src.at[at], dst.at[at], big.at[m, i]))
    for m, dst in enumerate((sg_ref, su_ref, sd_ref)):
        copies.append(pltpu.make_async_copy(scale_ref.at[m], dst, small.at[m]))
    copies.append(pltpu.make_async_copy(router_ref, out_router_ref, small.at[3]))
    for copy in copies:
        copy.start()
    for copy in copies:
        copy.wait()


def on_device(w_gate, avg_gate, w_up, avg_up, w_down, avg_down, router_weight, router_gain):
    n, ep = lax.axis_size("fsdp"), lax.axis_size("ep")
    experts, depth, d_expert = w_gate.shape
    span = w_down.shape[2]
    width = d_expert // n
    first, early = chunks_of(experts)
    rows = router_weight.shape[1]
    f32, bf16 = jnp.float32, jnp.bfloat16
    hbm = pl.BlockSpec(memory_space=pl.ANY)
    vmem = pl.BlockSpec(memory_space=pltpu.VMEM)
    shapes = (
        ((experts, n * depth, width), bf16),
        ((experts, n * depth, width), bf16),
        ((experts, width, n * span), bf16),
        ((3, experts, width), f32),
        ((ep, rows, n * depth), bf16),
    )
    counts = (first, early - first, 3 * experts - early)
    dma = pltpu.SemaphoreType.DMA
    work = pl.pallas_call(
        work_kernel,
        out_shape=[pltpu.VMEM(*shape) for shape in shapes],
        in_specs=[hbm] * 6 + [vmem] * 2,
        out_specs=[vmem] * 5,
        scratch_shapes=[
            pltpu.VMEM((SLOTS, depth, d_expert), f32),
            pltpu.VMEM((SLOTS, depth, d_expert), bf16),
            pltpu.VMEM((SLOTS, d_expert, span), f32),
            pltpu.VMEM((SLOTS, d_expert, span), bf16),
            pltpu.VMEM((RING, n, depth, width), bf16),
            pltpu.VMEM((RING, n, width, span), bf16),
            *[pltpu.VMEM((n, count, width), f32) for _ in range(3) for count in counts],
            pltpu.VMEM((rows, depth), bf16),
            dma((SLOTS, 2)),
            dma((SLOTS, 2)),
            dma((RING,)),
            dma((RING,)),
            dma((3, experts)),
            *[dma((3,)) for _ in range(4)],
            dma((2,)),
            dma((2,)),
        ],
        compiler_params=pltpu.CompilerParams(
            collective_id=0, has_side_effects=True, vmem_limit_bytes=30 * MIB
        ),
    )
    results = work(
        w_gate, avg_gate, w_up, avg_up, w_down, avg_down,
        router_weight.T, router_gain.reshape(1, depth),
    )
    outs = (
        shapes[0],
        shapes[1],
        shapes[2],
        ((experts, width), f32),
        ((experts, width), f32),
        ((experts, width), f32),
        shapes[4],
    )
    write = pl.pallas_call(
        write_kernel,
        out_shape=[jax.ShapeDtypeStruct(*shape) for shape in outs],
        in_specs=[vmem] * 5,
        out_specs=[hbm] * 7,
        scratch_shapes=[dma((3, min(4, experts))), dma((4,))],
        compiler_params=pltpu.CompilerParams(vmem_limit_bytes=4 * MIB),
    )
    *arrays, router = write(*results)
    return (*arrays, router.reshape(ep * rows, n * depth).T)


def solution(mesh):
    placed = (
        P("ep", "fsdp", None),
        P("ep", "fsdp", None),
        P("ep", "fsdp", None),
        P("ep", "fsdp", None),
        P("ep", None, "fsdp"),
        P("ep", None, "fsdp"),
        P("fsdp", "ep"),
        P("fsdp"),
    )
    return jax.shard_map(
        on_device,
        mesh=mesh,
        in_specs=placed,
        out_specs=(
            P("ep", None, "fsdp"),
            P("ep", None, "fsdp"),
            P("ep", "fsdp", None),
            P("ep", "fsdp"),
            P("ep", "fsdp"),
            P("ep", "fsdp"),
            P(),
        ),
        check_vma=False,
    )
```

time: 690 us -> 573 us (0.83)
  Pallas kernels: 75.9 us -> 572 us
  waiting for transfers between devices: 493 us -> 0 us
  local copies, waits for them, and re-layouts: 32.8 us -> 0 us
  starting transfers between devices: 25 us -> 0 us
  blocking collectives: 21.8 us -> 0 us
  other arithmetic: 21.7 us -> 0 us
  between operations: 14.1 us -> 0.64 us
    pallas_call x5 -> x2, Pallas kernels: 75.9 us -> 572 us  [the longest x1 564 us: on_device(): work(w_gate, avg_gate, w_up, avg_up, w_down, avg_down, router_weight.T, r...]
    all_to_all x3 -> x0, waiting for transfers between devices: 406 us -> none  [exchange(): return lax.all_to_all(x, 'fsdp', split_axis=0, concat_axis=0, tiled=True)]
    psum x2 -> x0, waiting for transfers between devices: 86.9 us -> none  [the longest x1 55 us: on_device(): total_up, total_down = lax.psum((square_up, square_down), 'fsdp')]
    all_to_all x3 -> x0, starting transfers between devices: 25 us -> none  [exchange(): return lax.all_to_all(x, 'fsdp', split_axis=0, concat_axis=0, tiled=True)]
    all_gather x2 -> x0, blocking collectives: 21.8 us -> none  [the longest x1 14.7 us: on_device(): row_router = lax.all_gather(part_router, 'fsdp', axis=0, tiled=True)]
    transpose x2 -> x0, local copies, waits for them, and re-layouts: 15.8 us -> none  [columns(): exchange(pieces).transpose(1, 0, 2, 3).reshape(experts, n * depth, width)]
    convert_element_type x2 -> x0, other arithmetic: 12 us -> none  [the longest x1 12 us: narrow_of(): (fresh_of(w, avg) / jnp.expand_dims(jnp.sqrt(total), axis)).astype(jnp.bf...]
    reshape x3 -> x0, local copies, waits for them, and re-layouts: 10.7 us -> none  [the longest x1 7.72 us: rows(): pieces = exchange(x.reshape(experts, n, part, depth).transpose(1, 0, 2, 3))]
  transfers between devices with their start and end apart: 5 -> 0, of which waited for: 5 -> 0; matrix products, arithmetic and copies ran while one was open for 7% -> 0% of each run, Pallas kernels for 5% -> 0%
where the time goes in v1:
time: 573 us
  Pallas kernels  572 us (100%)
    pallas_call x1, Pallas kernels, on_device(): work(w_gate, avg_gate, w_up, avg_up, w_down, avg_down, router_weight.T, r...  564 us

profile of v1, /device:TPU:9, one launch (start us, length us, event | category | flops | bytes accessed | tf_op | source)
XLA Modules:
  0.0 573.1 jit_solution(6816962019673748864)
XLA Ops:
  0.6 563.9 %shard_map.135 = (bf16[16,2048,128]{2,1,0:T(8,128)(2,1)S(1)}, bf16[16,2048,128]{2,1,0:T(8,128)(2,1)S(1)}, bf16[16,128,2048]{2,1,0:T(8,128)(2,1)S(1)}, f32[3,16,128]{2,1,0:T(8,128)S(1)}, bf16[4,16,2048]{2,1,0:T(8,128)(2,1)S(1)}) custom-call(f32[16,256,1024]{2,1,0:T(8,128)} %wg_ref.1, bf16[16,256,1024]{2,1,0:T(8,128)(2,1)} %ag_ref.1, f32[16,256,1024]{2,1,0:T(8,128)} %wu_ref.1, ...), custom_call_target="tpu_custom_call" | custom-call | tf_op jit(solution)/shard_map/pallas_call | solution.py:357
  564.6 8.5 %shard_map.136 = (bf16[16,2048,128]{2,1,0:T(8,128)(2,1)}, bf16[16,2048,128]{2,1,0:T(8,128)(2,1)}, bf16[16,128,2048]{2,1,0:T(8,128)(2,1)}, f32[16,128]{1,0:T(8,12...) custom-call(bf16[16,2048,128]{2,1,0:T(8,128)(2,1)S(1)} %get-tuple-element.19.g_ref, ...), custom_call_target="tpu_custom_call" | custom-call | tf_op jit(solution)/shard_map/pallas_call | solution.py:378

commit v2 on v1

--- a/solution.py
+++ b/solution.py
@@ -20,6 +20,10 @@
     return first, early
 
 
+def place_of(k, n):
+    return (k % 2) * (n // 2) + k // 2
+
+
 def fresh_of(w, avg):
     return w + avg.astype(jnp.float32)
 
@@ -28,15 +32,19 @@
     wg_ref, ag_ref, wu_ref, au_ref, wd_ref, ad_ref, rw_ref, gain_ref,
     og_ref, ou_ref, od_ref, scale_ref, router_ref,
     wide_w, wide_avg, tall_w, tall_avg, wide_stage, tall_stage,
-    part_a, part_b, part_c, sums_a, sums_b, sums_c, inv_a, inv_b, inv_c, own_router,
+    part_a, part_b, part_c, sums_a, sums_b, sums_c, inv_a, inv_b, inv_c, pair_c, own_router,
     wide_sem, tall_sem, wide_sent, tall_sent, landed,
-    sums_sent, sums_landed, inv_sent, inv_landed, router_sent, router_landed,
+    sums_sent, sums_landed, inv_sent, inv_landed, pair_sent, pair_landed,
+    router_sent, router_landed,
 ):
     n, ep = lax.axis_size("fsdp"), lax.axis_size("ep")
     me, group = lax.axis_index("fsdp"), lax.axis_index("ep")
     experts, depth, d_expert = wg_ref.shape
     width = d_expert // n
     first, early = chunks_of(experts)
+    half = n // 2
+    core, chip = lax.rem(me, 2), me // 2
+    place = core * half + chip
 
     barrier = pltpu.get_barrier_semaphore()
     for d in range(1, n):
@@ -86,7 +94,7 @@
         for k in range(n):
             at = slice(k * width, (k + 1) * width)
             fresh = fresh_of(wide_w[slot, :, at], wide_avg[slot, :, at])
-            part[k, pl.ds(e + shift, 1), :] = jnp.sum(fresh * fresh, axis=0, keepdims=True)
+            part[place_of(k, n), pl.ds(e + shift, 1), :] = jnp.sum(fresh * fresh, axis=0, keepdims=True)
 
     def row_sums(part, shift, e, slot):
         span = tall_w.shape[2]
@@ -97,48 +105,116 @@
                 lanes = slice(c * LANES, (c + 1) * LANES)
                 fresh = fresh_of(tall_w[slot, at, lanes], tall_avg[slot, at, lanes])
                 total = fresh * fresh if total is None else total + fresh * fresh
-            part[k, pl.ds(e + shift, 1), :] = jnp.sum(total.T, axis=0, keepdims=True)
+            part[place_of(k, n), pl.ds(e + shift, 1), :] = jnp.sum(total.T, axis=0, keepdims=True)
 
     def to_all(send):
         for d in range(1, n):
             send(lax.rem(me + d, n))
 
-    def send_sums(chunk, part, sums):
-        sums[me] = part[me]
+    def others(ref, sem, count=n - 1):
+        some = ref.at[pl.ds(0, count)]
+        return pltpu.make_async_copy(some, some, sem)
+
+    def remote(src, dst, sent, arrived, k):
+        return pltpu.make_async_remote_copy(
+            src_ref=src, dst_ref=dst, send_sem=sent, recv_sem=arrived,
+            device_id={"fsdp": k}, device_id_type=MESH,
+        )
+
+    def send_first():
+        sums_a[me] = part_a[...]
+        to_all(
+            lambda k: remote(
+                part_a, sums_a.at[me], sums_sent.at[0], sums_landed.at[0], k
+            ).start()
+        )
+
+    def take_first():
+        others(sums_a, sums_landed.at[0]).wait()
+
+        def total(of):
+            result = of(0)
+            for k in range(1, n):
+                result = result + of(k)
+            return result
+
+        scale_ref[0, 0:first] = jnp.sqrt(total(lambda k: sums_a[k, place]))
+        inv_a[...] = 1.0 / jnp.sqrt(total(lambda k: sums_a[k]))
+
+    def send_early():
+        sums_b[me] = part_b[place]
 
         def send(k):
-            pltpu.make_async_remote_copy(
-                src_ref=part.at[k], dst_ref=sums.at[me],
-                send_sem=sums_sent.at[chunk], recv_sem=sums_landed.at[chunk],
-                device_id={"fsdp": k}, device_id_type=MESH,
-            ).start()
+            at = lax.rem(k, 2) * half + k // 2
+            remote(part_b.at[at], sums_b.at[me], sums_sent.at[1], sums_landed.at[1], k).start()
 
         to_all(send)
 
-    def others(ref, sem):
-        some = ref.at[pl.ds(0, n - 1)]
-        return pltpu.make_async_copy(some, some, sem)
-
-    def send_inverse(chunk, sums, inv, places):
-        others(sums, sums_landed.at[chunk]).wait()
-        total = sums[0]
-        for k in range(1, n):
-            total = total + sums[k]
-        scale = jnp.sqrt(total)
+    def keep_scale(scale, places):
         at = 0
         for m, start, stop in places:
             scale_ref[m, start:stop] = scale[at : at + stop - start]
             at += stop - start
-        inv[me] = 1.0 / scale
-
-        def send(k):
-            pltpu.make_async_remote_copy(
-                src_ref=inv.at[me], dst_ref=inv.at[me],
-                send_sem=inv_sent.at[chunk], recv_sem=inv_landed.at[chunk],
-                device_id={"fsdp": k}, device_id_type=MESH,
+
+    def send_early_inverse():
+        others(sums_b, sums_landed.at[1]).wait()
+        total = sums_b[0]
+        for k in range(1, n):
+            total = total + sums_b[k]
+        scale = jnp.sqrt(total)
+        keep_scale(scale, ((0, first, early),))
+        inv_b[place] = 1.0 / scale
+        to_all(
+            lambda k: remote(
+                inv_b.at[place], inv_b.at[place], inv_sent.at[1], inv_landed.at[1], k
             ).start()
-
-        to_all(send)
+        )
+
+    def to_chips(send):
+        for d in range(1, half):
+            z = lax.rem(chip + d, half)
+            send(z, z * 2 + core)
+
+    sibling = me + 1 - 2 * core
+    theirs = pl.ds(pl.multiple_of((1 - core) * half, half), half)
+    ours = pl.ds(pl.multiple_of(core * half, half), half)
+
+    def send_rest():
+        copy = remote(part_c.at[theirs], pair_c, pair_sent.at[0], pair_landed.at[0], sibling)
+        copy.start()
+        copy.wait_recv()
+        part_c[ours] = part_c[ours] + pair_c[...]
+        sums_c[chip] = part_c[place]
+
+        def send(z, k):
+            remote(
+                part_c.at[core * half + z], sums_c.at[chip],
+                sums_sent.at[2], sums_landed.at[2], k,
+            ).start()
+
+        to_chips(send)
+
+    def send_rest_inverse(places):
+        if half > 1:
+            others(sums_c, sums_landed.at[2], half - 1).wait()
+        total = sums_c[0]
+        for z in range(1, half):
+            total = total + sums_c[z]
+        scale = jnp.sqrt(total)
+        keep_scale(scale, places)
+        inv_c[place] = 1.0 / scale
+        to_chips(
+            lambda z, k: remote(
+                inv_c.at[place], inv_c.at[place], inv_sent.at[2], inv_landed.at[2], k
+            ).start()
+        )
+
+    def share_rest_inverse():
+        if half > 1:
+            others(inv_c, inv_landed.at[2], half - 1).wait()
+        copy = remote(inv_c.at[ours], inv_c.at[ours], pair_sent.at[1], pair_landed.at[1], sibling)
+        copy.start()
+        copy.wait_recv()
 
     def ring_slot(stage, sent, count):
         ring = lax.rem(count, RING)
@@ -154,7 +230,7 @@
         for k in range(n):
             at = slice(k * width, (k + 1) * width)
             fresh = fresh_of(wide_w[slot, :, at], wide_avg[slot, :, at])
-            wide_stage[ring, k] = (fresh * inv[k, pl.ds(e + shift, 1), :]).astype(jnp.bfloat16)
+            wide_stage[ring, k] = (fresh * inv[place_of(k, n), pl.ds(e + shift, 1), :]).astype(jnp.bfloat16)
         rows = pl.ds(pl.multiple_of(me * depth, depth), depth)
 
         def send(k):
@@ -172,7 +248,7 @@
         span = tall_w.shape[2]
         for k in range(n):
             at = slice(k * width, (k + 1) * width)
-            row = inv[k, pl.ds(e + shift, 1), :]
+            row = inv[place_of(k, n), pl.ds(e + shift, 1), :]
             factor = jnp.broadcast_to(row, (LANES, width)).T
             for c in range(span // LANES):
                 lanes = slice(c * LANES, (c + 1) * LANES)
@@ -190,52 +266,57 @@
         to_all(send)
         od_ref[e, :, columns] = tall_stage[ring, me]
 
-    prime(gate, 0, first)
-    own_router[...] = (rw_ref[...] * gain_ref[...]).astype(jnp.bfloat16)
-    pl.semaphore_wait(barrier, n - 1 + ep - 1)
-
-    stream(gate, 0, first, functools.partial(column_sums, part_a, 0))
-    prime(gate, first, early)
-    send_sums(0, part_a, sums_a)
-    stream(gate, first, early, functools.partial(column_sums, part_b, -first))
-    prime(gate, 0, first)
-    send_sums(1, part_b, sums_b)
-    send_inverse(0, sums_a, inv_a, ((0, 0, first),))
-
     my_columns = pl.ds(pl.multiple_of(me * depth, depth), depth)
-
-    def send_router(k):
-        pltpu.make_async_remote_copy(
-            src_ref=own_router, dst_ref=router_ref.at[group, :, my_columns],
-            send_sem=router_sent.at[0], recv_sem=router_landed.at[0],
-            device_id={"fsdp": k}, device_id_type=MESH,
-        ).start()
 
     def router_wait(sem):
         some = router_ref.at[group, :, pl.ds(0, (n - 1) * depth)]
         return pltpu.make_async_copy(some, some, sem)
 
-    send_inverse(1, sums_b, inv_b, ((0, first, early),))
-    others(inv_a, inv_landed.at[0]).wait()
-    stream(gate, 0, first, functools.partial(wide_pieces, 0, og_ref, inv_a, 0))
+    for e in range(first):
+        for copy in loads(gate, e, SLOTS + e):
+            copy.start()
+    own_router[...] = (rw_ref[...] * gain_ref[...]).astype(jnp.bfloat16)
+    router_ref[group, :, my_columns] = own_router[...]
+    for e in range(first):
+        for copy in loads(gate, e, SLOTS + e):
+            copy.wait()
+    prime(gate, first, early)
+    for e in range(first):
+        column_sums(part_a, 0, e, SLOTS + e)
+    pl.semaphore_wait(barrier, n - 1 + ep - 1)
+    send_first()
+    stream(gate, first, early, functools.partial(column_sums, part_b, -first))
+    send_early()
+    to_all(
+        lambda k: remote(
+            own_router, router_ref.at[group, :, my_columns],
+            router_sent.at[0], router_landed.at[0], k,
+        ).start()
+    )
+    prime(gate, early, experts)
+    prime(down, 0, experts)
+
+    take_first()
+    wide_pieces(0, og_ref, inv_a, 0, 0, SLOTS)
+    send_early_inverse()
+    for e in range(1, first):
+        wide_pieces(0, og_ref, inv_a, 0, e, SLOTS + e)
+
+    rest = experts - early
+    stream(gate, early, experts, functools.partial(column_sums, part_c, -early))
+    prime(up, 0, experts)
+    stream(up, 0, experts, functools.partial(column_sums, part_c, rest))
+
     pieces_b = functools.partial(wide_pieces, 0, og_ref, inv_b, -first)
-    cut_one = first + (early - first + 2) // 3
+    cut_one = first + (early - first + 1) // 2
     cut_two = cut_one + (early - cut_one + 1) // 2
     prime(gate, first, cut_one)
     others(inv_b, inv_landed.at[1]).wait()
     stream(gate, first, cut_one, pieces_b)
-    to_all(send_router)
-    router_ref[group, :, my_columns] = own_router[...]
-
-    prime(gate, early, experts)
-    prime(down, 0, experts)
-    stream(gate, early, experts, functools.partial(column_sums, part_c, -early))
-    rest = experts - early
-    prime(up, 0, experts)
-    stream(up, 0, experts, functools.partial(column_sums, part_c, rest))
+
     stream(down, 0, experts, functools.partial(row_sums, part_c, rest + experts))
-    send_sums(2, part_c, sums_c)
     prime(gate, cut_one, cut_two)
+    send_rest()
     stream(gate, cut_one, cut_two, pieces_b)
 
     router_wait(router_landed.at[0]).wait()
@@ -246,27 +327,27 @@
             device_id={"ep": lax.rem(group + d, ep)}, device_id_type=MESH,
         ).start()
 
-    send_inverse(
-        2, sums_c, inv_c, ((0, early, experts), (1, 0, experts), (2, 0, experts))
-    )
     prime(gate, cut_two, early)
+    send_rest_inverse(((0, early, experts), (1, 0, experts), (2, 0, experts)))
     stream(gate, cut_two, early, pieces_b)
     prime(gate, early, experts)
     prime(down, 0, experts)
-    others(inv_c, inv_landed.at[2]).wait()
+    share_rest_inverse()
     stream(gate, early, experts, functools.partial(wide_pieces, 0, og_ref, inv_c, -early))
     prime(up, 0, experts)
     stream(up, 0, experts, functools.partial(wide_pieces, 1, ou_ref, inv_c, rest))
     stream(down, 0, experts, functools.partial(tall_pieces, inv_c, rest + experts))
 
-    def finish(e, carry):
-        wide = wide_stage.at[0, pl.ds(0, n - 1)]
-        tall = tall_stage.at[0, pl.ds(0, n - 1)]
-        for m, some in ((0, wide), (1, wide), (2, tall)):
-            pltpu.make_async_copy(some, some, landed.at[m, e]).wait()
-        return carry
-
-    lax.fori_loop(0, experts, finish, 0)
+    def arrived(m, e):
+        stage = tall_stage if m == 2 else wide_stage
+        others(stage.at[0], landed.at[m, e]).wait()
+
+    def finish(m):
+        def step(e, carry):
+            arrived(m, e)
+            return carry
+
+        lax.fori_loop(0, experts, step, 0)
 
     def drain(count, stage, sent):
         def step(i, carry):
@@ -275,16 +356,24 @@
 
         lax.fori_loop(0, min(RING, count), step, 0)
 
-    drain(2 * experts, wide_stage, wide_sent)
-    drain(experts, tall_stage, tall_sent)
-    for chunk, (part, inv) in enumerate(((part_a, inv_a), (part_b, inv_b), (part_c, inv_c))):
-        others(part, sums_sent.at[chunk]).wait()
-        others(inv, inv_sent.at[chunk]).wait()
+    others(sums_a, sums_sent.at[0]).wait()
+    others(part_b, sums_sent.at[1]).wait()
+    others(inv_b, inv_sent.at[1]).wait()
+    if half > 1:
+        others(sums_c, sums_sent.at[2], half - 1).wait()
+        others(inv_c, inv_sent.at[2], half - 1).wait()
+    others(pair_c, pair_sent.at[0], half).wait()
+    others(inv_c, pair_sent.at[1], half).wait()
     router_wait(router_sent.at[0]).wait()
     if ep > 1:
         some = router_ref.at[pl.ds(0, ep - 1)]
         pltpu.make_async_copy(some, some, router_sent.at[1]).wait()
         pltpu.make_async_copy(some, some, router_landed.at[1]).wait()
+    finish(0)
+    finish(1)
+    drain(2 * experts, wide_stage, wide_sent)
+    drain(experts, tall_stage, tall_sent)
+    finish(2)
 
 
 def write_kernel(
@@ -333,22 +422,26 @@
         in_specs=[hbm] * 6 + [vmem] * 2,
         out_specs=[vmem] * 5,
         scratch_shapes=[
-            pltpu.VMEM((SLOTS, depth, d_expert), f32),
-            pltpu.VMEM((SLOTS, depth, d_expert), bf16),
+            pltpu.VMEM((SLOTS + first, depth, d_expert), f32),
+            pltpu.VMEM((SLOTS + first, depth, d_expert), bf16),
             pltpu.VMEM((SLOTS, d_expert, span), f32),
             pltpu.VMEM((SLOTS, d_expert, span), bf16),
             pltpu.VMEM((RING, n, depth, width), bf16),
             pltpu.VMEM((RING, n, width, span), bf16),
-            *[pltpu.VMEM((n, count, width), f32) for _ in range(3) for count in counts],
+            *[pltpu.VMEM((n, count, width), f32) for count in counts],
+            pltpu.VMEM((n, n, first, width), f32),
+            pltpu.VMEM((n, counts[1], width), f32),
+            pltpu.VMEM((n // 2, counts[2], width), f32),
+            *[pltpu.VMEM((n, count, width), f32) for count in counts],
+            pltpu.VMEM((n // 2, counts[2], width), f32),
             pltpu.VMEM((rows, depth), bf16),
-            dma((SLOTS, 2)),
+            dma((SLOTS + first, 2)),
             dma((SLOTS, 2)),
             dma((RING,)),
             dma((RING,)),
             dma((3, experts)),
             *[dma((3,)) for _ in range(4)],
-            dma((2,)),
-            dma((2,)),
+            *[dma((2,)) for _ in range(4)],
         ],
         compiler_params=pltpu.CompilerParams(
             collective_id=0, has_side_effects=True, vmem_limit_bytes=30 * MIB

time: 573 us -> 565 us (0.986)
  Pallas kernels: 572 us -> 564 us
    pallas_call x1, Pallas kernels: 564 us -> 556 us  [on_device(): work(w_gate, avg_gate, w_up, avg_up, w_down, avg_down, router_weight.T, r...]
where the time goes in v2:
time: 565 us
  Pallas kernels  564 us (100%)
    pallas_call x1, Pallas kernels, on_device(): work(w_gate, avg_gate, w_up, avg_up, w_down, avg_down, router_weight.T, r...  556 us

profile of v2, /device:TPU:9, one launch (start us, length us, event | category | flops | bytes accessed | tf_op | source)
XLA Modules:
  0.0 565.0 jit_solution(739817226251693438)
XLA Ops:
  0.6 555.8 %shard_map.135 = (bf16[16,2048,128]{2,1,0:T(8,128)(2,1)S(1)}, bf16[16,2048,128]{2,1,0:T(8,128)(2,1)S(1)}, bf16[16,128,2048]{2,1,0:T(8,128)(2,1)S(1)}, f32[3,16,128]{2,1,0:T(8,128)S(1)}, bf16[4,16,2048]{2,1,0:T(8,128)(2,1)S(1)}) custom-call(f32[16,256,1024]{2,1,0:T(8,128)} %wg_ref.1, bf16[16,256,1024]{2,1,0:T(8,128)(2,1)} %ag_ref.1, f32[16,256,1024]{2,1,0:T(8,128)} %wu_ref.1, ...), custom_call_target="tpu_custom_call" | custom-call | tf_op jit(solution)/shard_map/pallas_call | solution.py:450
  556.4 8.5 %shard_map.136 = (bf16[16,2048,128]{2,1,0:T(8,128)(2,1)}, bf16[16,2048,128]{2,1,0:T(8,128)(2,1)}, bf16[16,128,2048]{2,1,0:T(8,128)(2,1)}, f32[16,128]{1,0:T(8,12...) custom-call(bf16[16,2048,128]{2,1,0:T(8,128)(2,1)S(1)} %get-tuple-element.19.g_ref, ...), custom_call_target="tpu_custom_call" | custom-call | tf_op jit(solution)/shard_map/pallas_call | solution.py:471

commit v3 on v2

--- a/solution.py
+++ b/solution.py
@@ -16,12 +16,17 @@
 
 def chunks_of(experts):
     first = max(1, experts // 8)
-    early = max(first, experts // 2)
+    early = max(first + 1, experts * 3 // 8)
     return first, early
 
 
 def place_of(k, n):
-    return (k % 2) * (n // 2) + k // 2
+    chip, place, width = k // 2, 0, n // 2
+    while width > 1:
+        width //= 2
+        place = place + (chip % 2) * width
+        chip = chip // 2
+    return (k % 2) * (n // 2) + place
 
 
 def fresh_of(w, avg):
@@ -44,7 +49,8 @@
     first, early = chunks_of(experts)
     half = n // 2
     core, chip = lax.rem(me, 2), me // 2
-    place = core * half + chip
+    place = place_of(me, n)
+    steps = half.bit_length() - 1
 
     barrier = pltpu.get_barrier_semaphore()
     for d in range(1, n):
@@ -145,8 +151,7 @@
         sums_b[me] = part_b[place]
 
         def send(k):
-            at = lax.rem(k, 2) * half + k // 2
-            remote(part_b.at[at], sums_b.at[me], sums_sent.at[1], sums_landed.at[1], k).start()
+            remote(part_b.at[place_of(k, n)], sums_b.at[me], sums_sent.at[1], sums_landed.at[1], k).start()
 
         to_all(send)
 
@@ -170,10 +175,9 @@
             ).start()
         )
 
-    def to_chips(send):
-        for d in range(1, half):
-            z = lax.rem(chip + d, half)
-            send(z, z * 2 + core)
+    def across(step):
+        bit = chip // (1 << step) % 2
+        return bit, (chip + (1 - 2 * bit) * (1 << step)) * 2 + core
 
     sibling = me + 1 - 2 * core
     theirs = pl.ds(pl.multiple_of((1 - core) * half, half), half)
@@ -184,34 +188,45 @@
         copy.start()
         copy.wait_recv()
         part_c[ours] = part_c[ours] + pair_c[...]
-        sums_c[chip] = part_c[place]
-
-        def send(z, k):
-            remote(
-                part_c.at[core * half + z], sums_c.at[chip],
-                sums_sent.at[2], sums_landed.at[2], k,
-            ).start()
-
-        to_chips(send)
-
-    def send_rest_inverse(places):
-        if half > 1:
-            others(sums_c, sums_landed.at[2], half - 1).wait()
-        total = sums_c[0]
-        for z in range(1, half):
-            total = total + sums_c[z]
-        scale = jnp.sqrt(total)
+
+    def halving(step):
+        size = half >> (step + 1)
+        base = core * half
+        for before in range(step):
+            base = base + across(before)[0] * (half >> (before + 1))
+        bit, partner = across(step)
+        keep, give = base + bit * size, base + (1 - bit) * size
+        inbox = pl.ds(half - 2 * size, size)
+        copy = remote(
+            part_c.at[pl.ds(give, size)], sums_c.at[inbox],
+            sums_sent.at[2 + step], sums_landed.at[2 + step], partner,
+        )
+        return copy, pl.ds(keep, size), inbox
+
+    def send_half(step):
+        halving(step)[0].start()
+
+    def take_half(step):
+        copy, keep, inbox = halving(step)
+        copy.wait_recv()
+        part_c[keep] = part_c[keep] + sums_c[inbox]
+
+    def make_rest_inverse(places):
+        scale = jnp.sqrt(part_c[place])
         keep_scale(scale, places)
         inv_c[place] = 1.0 / scale
-        to_chips(
-            lambda z, k: remote(
-                inv_c.at[place], inv_c.at[place], inv_sent.at[2], inv_landed.at[2], k
-            ).start()
+
+    def doubling(step):
+        size = half >> (step + 1)
+        base = core * half
+        for before in range(step + 1):
+            base = base + across(before)[0] * (half >> (before + 1))
+        some = inv_c.at[pl.ds(base, size)]
+        return remote(
+            some, some, inv_sent.at[2 + step], inv_landed.at[2 + step], across(step)[1]
         )
 
     def share_rest_inverse():
-        if half > 1:
-            others(inv_c, inv_landed.at[2], half - 1).wait()
         copy = remote(inv_c.at[ours], inv_c.at[ours], pair_sent.at[1], pair_landed.at[1], sibling)
         copy.start()
         copy.wait_recv()
@@ -309,15 +324,20 @@
 
     pieces_b = functools.partial(wide_pieces, 0, og_ref, inv_b, -first)
     cut_one = first + (early - first + 1) // 2
-    cut_two = cut_one + (early - cut_one + 1) // 2
     prime(gate, first, cut_one)
     others(inv_b, inv_landed.at[1]).wait()
     stream(gate, first, cut_one, pieces_b)
 
     stream(down, 0, experts, functools.partial(row_sums, part_c, rest + experts))
-    prime(gate, cut_one, cut_two)
     send_rest()
-    stream(gate, cut_one, cut_two, pieces_b)
+    turns = 2 * steps
+    cuts = [cut_one + (early - cut_one) * i // max(1, turns) for i in range(turns + 1)]
+    for step in range(steps):
+        send_half(step)
+        prime(gate, cuts[step], cuts[step + 1])
+        stream(gate, cuts[step], cuts[step + 1], pieces_b)
+        take_half(step)
+    make_rest_inverse(((0, early, experts), (1, 0, experts), (2, 0, experts)))
 
     router_wait(router_landed.at[0]).wait()
     for d in range(1, ep):
@@ -327,9 +347,11 @@
             device_id={"ep": lax.rem(group + d, ep)}, device_id_type=MESH,
         ).start()
 
-    prime(gate, cut_two, early)
-    send_rest_inverse(((0, early, experts), (1, 0, experts), (2, 0, experts)))
-    stream(gate, cut_two, early, pieces_b)
+    for turn, step in enumerate(reversed(range(steps)), steps):
+        doubling(step).start()
+        prime(gate, cuts[turn], cuts[turn + 1])
+        stream(gate, cuts[turn], cuts[turn + 1], pieces_b)
+        doubling(step).wait_recv()
     prime(gate, early, experts)
     prime(down, 0, experts)
     share_rest_inverse()
@@ -359,9 +381,9 @@
     others(sums_a, sums_sent.at[0]).wait()
     others(part_b, sums_sent.at[1]).wait()
     others(inv_b, inv_sent.at[1]).wait()
-    if half > 1:
-        others(sums_c, sums_sent.at[2], half - 1).wait()
-        others(inv_c, inv_sent.at[2], half - 1).wait()
+    for step in range(steps):
+        halving(step)[0].wait_send()
+        doubling(step).wait_send()
     others(pair_c, pair_sent.at[0], half).wait()
     others(inv_c, pair_sent.at[1], half).wait()
     router_wait(router_sent.at[0]).wait()
@@ -431,7 +453,7 @@
             *[pltpu.VMEM((n, count, width), f32) for count in counts],
             pltpu.VMEM((n, n, first, width), f32),
             pltpu.VMEM((n, counts[1], width), f32),
-            pltpu.VMEM((n // 2, counts[2], width), f32),
+            pltpu.VMEM((max(1, n // 2 - 1), counts[2], width), f32),
             *[pltpu.VMEM((n, count, width), f32) for count in counts],
             pltpu.VMEM((n // 2, counts[2], width), f32),
             pltpu.VMEM((rows, depth), bf16),
@@ -440,7 +462,7 @@
             dma((RING,)),
             dma((RING,)),
             dma((3, experts)),
-            *[dma((3,)) for _ in range(4)],
+            *[dma((2 + n.bit_length(),)) for _ in range(4)],
             *[dma((2,)) for _ in range(4)],
         ],
         compiler_params=pltpu.CompilerParams(

time: 565 us -> 564 us (level)
  no operation moved by 1% of the time
where the time goes in v3:
time: 564 us; the launch traced here: 562 us
  Pallas kernels  562 us (100%)
    pallas_call x1, Pallas kernels, on_device(): work(w_gate, avg_gate, w_up, avg_up, w_down, avg_down, router_weight.T, r...  553 us

profile of v3, /device:TPU:9, one launch (start us, length us, event | category | flops | bytes accessed | tf_op | source)
XLA Modules:
  0.0 562.2 jit_solution(12931612456053792990)
XLA Ops:
  0.6 553.0 %shard_map.135 = (bf16[16,2048,128]{2,1,0:T(8,128)(2,1)S(1)}, bf16[16,2048,128]{2,1,0:T(8,128)(2,1)S(1)}, bf16[16,128,2048]{2,1,0:T(8,128)(2,1)S(1)}, f32[3,16,128]{2,1,0:T(8,128)S(1)}, bf16[4,16,2048]{2,1,0:T(8,128)(2,1)S(1)}) custom-call(f32[16,256,1024]{2,1,0:T(8,128)} %wg_ref.1, bf16[16,256,1024]{2,1,0:T(8,128)(2,1)} %ag_ref.1, f32[16,256,1024]{2,1,0:T(8,128)} %wu_ref.1, ...), custom_call_target="tpu_custom_call" | custom-call | tf_op jit(solution)/shard_map/pallas_call | solution.py:472
  553.6 8.5 %shard_map.136 = (bf16[16,2048,128]{2,1,0:T(8,128)(2,1)}, bf16[16,2048,128]{2,1,0:T(8,128)(2,1)}, bf16[16,128,2048]{2,1,0:T(8,128)(2,1)}, f32[16,128]{1,0:T(8,12...) custom-call(bf16[16,2048,128]{2,1,0:T(8,128)(2,1)S(1)} %get-tuple-element.19.g_ref, ...), custom_call_target="tpu_custom_call" | custom-call | tf_op jit(solution)/shard_map/pallas_call | solution.py:493

commit v4 on v3

--- a/solution.py
+++ b/solution.py
@@ -114,8 +114,9 @@
             part[place_of(k, n), pl.ds(e + shift, 1), :] = jnp.sum(total.T, axis=0, keepdims=True)
 
     def to_all(send):
+        way = 2 * (me // half) - 1
         for d in range(1, n):
-            send(lax.rem(me + d, n))
+            send(lax.rem(me + way * d + n, n))
 
     def others(ref, sem, count=n - 1):
         some = ref.at[pl.ds(0, count)]

time: 564 us -> 562 us (level)
  no operation moved by 1% of the time
where the time goes in v4:
time: 562 us
  Pallas kernels  561 us (100%)
    pallas_call x1, Pallas kernels, on_device(): work(w_gate, avg_gate, w_up, avg_up, w_down, avg_down, router_weight.T, r...  553 us

profile of v4, /device:TPU:9, one launch (start us, length us, event | category | flops | bytes accessed | tf_op | source)
XLA Modules:
  0.0 561.9 jit_solution(2277016157983476108)
XLA Ops:
  0.6 552.7 %shard_map.135 = (bf16[16,2048,128]{2,1,0:T(8,128)(2,1)S(1)}, bf16[16,2048,128]{2,1,0:T(8,128)(2,1)S(1)}, bf16[16,128,2048]{2,1,0:T(8,128)(2,1)S(1)}, f32[3,16,128]{2,1,0:T(8,128)S(1)}, bf16[4,16,2048]{2,1,0:T(8,128)(2,1)S(1)}) custom-call(f32[16,256,1024]{2,1,0:T(8,128)} %wg_ref.1, bf16[16,256,1024]{2,1,0:T(8,128)(2,1)} %ag_ref.1, f32[16,256,1024]{2,1,0:T(8,128)} %wu_ref.1, ...), custom_call_target="tpu_custom_call" | custom-call | tf_op jit(solution)/shard_map/pallas_call | solution.py:473
  553.4 8.5 %shard_map.136 = (bf16[16,2048,128]{2,1,0:T(8,128)(2,1)}, bf16[16,2048,128]{2,1,0:T(8,128)(2,1)}, bf16[16,128,2048]{2,1,0:T(8,128)(2,1)}, f32[16,128]{1,0:T(8,12...) custom-call(bf16[16,2048,128]{2,1,0:T(8,128)(2,1)S(1)} %get-tuple-element.19.g_ref, ...), custom_call_target="tpu_custom_call" | custom-call | tf_op jit(solution)/shard_map/pallas_call | solution.py:494
